TPU v7x, 32 devices: a whole 2x2x4 slice. The times are simulated.
32 devices in a mesh: groups: 2 (over y), rows: 4 (over z), cols: 2 (over x), sub: 2 (over core).
Axes of the slice: x: 2, y: 2, z: 4, core: 2. Of those that a mesh axis runs over, the one named last changes fastest.
Arguments:
- stored_vectors: bfloat16 [3072, 8192], P(('cols', 'sub'), ('groups', 'rows')), parts along dimension 1, may hold values from -0.59765625 to 0.59765625
- previous_columns: bfloat16 [8192, 256], P(('groups', 'rows', 'cols', 'sub')), parts along dimension 0, may hold values from -3 to 3
- pivots: int32 [512], P('groups'), parts along dimension 0, may hold values from 0 to 4095, as said below
- diagonal: float32 [8192], P(('groups', 'rows', 'cols', 'sub')), parts along dimension 0, may hold values from 2 to 32
- ket_blocks: bfloat16 [128, 128, 256], P(('groups', 'rows', 'cols', 'sub')), parts along dimension 0, may hold values from -6 to 6
- shell_tags: int32 [128, 128], P(('groups', 'rows', 'cols', 'sub')), parts along dimension 0, may hold values from 0 to 3
- target_blocks: int32 [32, 4], P('groups'), parts along dimension 0, may hold values from 0 to 31, as said below
- block_counts: int32 [32], P('groups'), parts along dimension 0, may hold values from 0 to 4, as said below
- shell_norms: float32 [4], replicated, may hold values from 0.5 to 2
Outputs:
- new_vectors: bfloat16 [8192, 256], P(('groups', 'rows', 'cols', 'sub')), parts along dimension 0
- diag_out: float32 [8192], P(('groups', 'rows', 'cols', 'sub')), parts along dimension 0
- next_columns: bfloat16 [8192, 256], P(('groups', 'rows', 'cols', 'sub')), parts along dimension 0
There are 2 independent parts, one for each index of `groups`. A program takes and returns all parts, laid end to end along the dimension named above; an argument that names none is the same for every part. Nothing has to cross between parts.
Inputs may be any that keep to these rules, and one draw needn't show every extreme that they name: `pivots`: 256 distinct AO pairs. `target_blocks`: the used slots of all owners name every block of the 32 blocks exactly once; a used slot's block lies on a device with the owner's cols and sub indices (blocks g * 2 to g * 2 + 1 lie on the device of linear index g, rows slowest; owner o is the device of linear index o). At most 1 of one owner's used slots go to one device, and some owner reaches that in every draw. Entries of unused slots are arbitrary blocks. `block_counts`: some owner uses all 4 slots in every draw.
All inputs are finite; a program needn't handle non-finite values.
Results may differ from a plain program's by a relative error of at most 0.0004.
Values may be sent and summed in bfloat16 or wider, within the bound.
A program may use at most 64 MiB of HBM per device.

v0:
```python
import jax
import jax.numpy as jnp
from jax import lax
from jax.sharding import PartitionSpec as P


def slot_plan(row_targets, count, column_size, per_device):
    slot_count = row_targets.shape[0]
    slots = jnp.arange(slot_count, dtype=jnp.int32)
    valid = slots < count
    receiver = row_targets // (column_size * per_device)
    within = row_targets % per_device
    earlier = (
        (receiver[:, None] == receiver[None, :])
        & valid[:, None]
        & valid[None, :]
        & (slots[None, :] < slots[:, None])
    )
    ranking = jnp.sum(earlier.astype(jnp.int32), axis=1)
    return (valid, receiver, ranking, within)


def body(
    stored_vectors,
    previous_columns,
    pivots,
    diagonal,
    ket_blocks,
    shell_tags,
    target_blocks,
    block_counts,
    shell_norms,
):
    rows_here = previous_columns.shape[0]
    batch = previous_columns.shape[1]
    block_rows = ket_blocks.shape[1]
    slot_count = ket_blocks.shape[0]
    per_device = rows_here // block_rows
    band_rows = stored_vectors.shape[1]
    band_index = lax.axis_index("rows")
    device_index = lax.axis_index(("rows", "cols", "sub"))
    column_index = lax.axis_index(("cols", "sub"))
    column_size = lax.axis_size(("cols", "sub"))
    band_size = lax.axis_size("rows")
    peer_slots = (slot_count + band_size - 1) // band_size
    local_pivots = pivots - device_index * rows_here
    matches = jnp.arange(rows_here, dtype=jnp.int32)[:, None] == local_pivots[None, :]
    diag_terms = jnp.sum(jnp.where(matches, diagonal[:, None], jnp.float32(0.0)), axis=0)
    pivot_diag = lax.psum(diag_terms, ("rows", "cols", "sub"))
    band_pivots = pivots - band_index * band_rows
    inside = (band_pivots >= 0) & (band_pivots < band_rows)
    clamped = jnp.clip(band_pivots, 0, band_rows - 1)
    taken = jnp.take(stored_vectors, clamped, axis=1).astype(jnp.float32)
    picked = jnp.where(inside[None, :], taken, jnp.float32(0.0))
    pivot_rows = lax.psum(picked, "rows").astype(jnp.bfloat16)
    kinds = jnp.arange(shell_norms.shape[0], dtype=jnp.int32)
    factor = jnp.sum(
        jnp.where(shell_tags[..., None] == kinds, shell_norms, jnp.float32(0.0)), axis=-1
    )
    fresh = (ket_blocks.astype(jnp.float32) * factor[..., None]).astype(jnp.bfloat16)
    own_targets = lax.dynamic_index_in_dim(target_blocks, device_index, 0, keepdims=False)
    own_count = lax.dynamic_index_in_dim(block_counts, device_index, 0, keepdims=False)
    valid, receiver, ranking, within = slot_plan(own_targets, own_count, column_size, per_device)
    lines = jnp.arange(band_size * peer_slots, dtype=jnp.int32)[:, None]
    routing = (
        (lines // peer_slots == receiver[None, :])
        & (lines % peer_slots == ranking[None, :])
        & valid[None, :]
    ).astype(jnp.bfloat16)
    outgoing = jnp.dot(
        routing, fresh.reshape(slot_count, block_rows * batch), preferred_element_type=jnp.float32
    )
    outgoing = outgoing.astype(jnp.bfloat16).reshape(band_size, peer_slots, block_rows, batch)
    incoming = lax.all_to_all(outgoing, "rows", split_axis=0, concat_axis=0, tiled=True)
    sources = jnp.arange(band_size, dtype=jnp.int32) * column_size + column_index
    source_targets = jnp.take(target_blocks, sources, axis=0)
    source_counts = jnp.take(block_counts, sources, axis=0)
    plan_each = jax.vmap(
        lambda row_targets, count: slot_plan(row_targets, count, column_size, per_device)
    )
    source_valid, source_receiver, source_rank, source_within = plan_each(
        source_targets, source_counts
    )
    arriving = source_valid & (source_receiver == band_index)
    places = jnp.arange(per_device, dtype=jnp.int32)[:, None, None, None]
    peer_lines = jnp.arange(peer_slots, dtype=jnp.int32)[None, None, :, None]
    hits = (
        (source_within[None, :, None, :] == places)
        & (source_rank[None, :, None, :] == peer_lines)
        & arriving[None, :, None, :]
    )
    placement = (
        jnp.any(hits, axis=3).astype(jnp.bfloat16).reshape(per_device, band_size * peer_slots)
    )
    arranged = jnp.dot(
        placement,
        incoming.reshape(band_size * peer_slots, block_rows * batch),
        preferred_element_type=jnp.float32,
    )
    next_columns = arranged.astype(jnp.bfloat16).reshape(rows_here, batch)
    product = lax.psum_scatter(
        lax.dot_general(
            stored_vectors, pivot_rows, (((0,), (0,)), ((), ())), preferred_element_type=jnp.float32
        ),
        ("cols", "sub"),
        scatter_dimension=0,
        tiled=True,
    )
    residual_cols = previous_columns.astype(jnp.float32) - product
    scaled = residual_cols / jnp.sqrt(pivot_diag)[None, :]
    new_vectors = scaled.astype(jnp.bfloat16)
    diag_out = diagonal - jnp.sum(scaled * scaled, axis=1)
    return (new_vectors, diag_out, next_columns)


def solution(mesh):
    return jax.shard_map(
        body,
        mesh=mesh,
        in_specs=(
            P(("cols", "sub"), ("groups", "rows")),
            P(("groups", "rows", "cols", "sub"), None),
            P("groups"),
            P(("groups", "rows", "cols", "sub")),
            P(("groups", "rows", "cols", "sub"), None, None),
            P(("groups", "rows", "cols", "sub"), None),
            P("groups", None),
            P("groups"),
            P(),
        ),
        out_specs=(
            P(("groups", "rows", "cols", "sub"), None),
            P(("groups", "rows", "cols", "sub")),
            P(("groups", "rows", "cols", "sub"), None),
        ),
        check_vma=False,
    )
```

profile of v0, /device:TPU:0, one launch (start us, length us, event | category | flops | bytes accessed | tf_op | source)
XLA Modules:
  0.0 100.1 jit_solution(16816415105481037228)
XLA Ops:
  7.2 0.0 reduce-scatter.2.cloned.1.call-start
  7.2 0.0 copy-start.6
  7.2 1.7 %copy.26 = bf16[768,1024]{0,1:T(8,128)(2,1)S(1)} copy(bf16[768,1024]{1,0:T(8,128)(2,1)} %param.9) | data formatting | bytes 3145728 | tf_op args[0]
  9.0 0.0 copy-done.6
  9.0 1.2 %gather_fusion = bf16[256,768]{1,0:T(8,128)(2,1)S(1)} fusion(bf16[768,1024]{0,1:T(8,128)(2,1)S(1)} %copy.26, s32[1024]{0:T(1024)S(1)} %pad_clamp_fusion.1), kind=kCustom, calls=%fused_computation | custom fusion | bytes 787456 | tf_op jit(solution)/shard_map/jit(_take)/gather | solution.py:53
  10.2 0.0 copy-start.1
  10.2 0.2 select_bitcast_fusion
  10.4 37.4 %all-reduce.1 = bf16[768,256]{0,1:T(8,128)(2,1)S(1)} all-reduce(f32[768,256]{0,1:T(8,128)S(1)} %select_bitcast_fusion), channel_id=1, replica_groups=mesh['groups'=2,'rows'=4,'cols'=2,'sub'=2] {'rows'}, use_global_device_ids=true, to_apply=%region_0.1 | all-reduce | flops 196608 | bytes 1179648 | tf_op jit(solution)/shard_map/psum | solution.py:55
  47.8 0.0 copy-done.1
  47.8 0.0 copy-start.7
  47.8 0.0 copy-start.8
  47.9 0.0 copy-start.2
  47.9 1.6 %convolution_bitcast_fusion = f32[1024,256]{0,1:T(8,128)} fusion(bf16[768,1024]{1,0:T(8,128)(2,1)S(1)} %copy-done.1, bf16[768,256]{0,1:T(8,128)(2,1)S(1)} %all-reduce.1), kind=kOutput, calls=%fused_computation.5 | convolution fusion | flops 402653184 | bytes 3014656 | tf_op jit(solution)/shard_map/dot_general | solution.py:102
  49.4 0.0 copy-start.4
  49.4 0.0 copy-start
  49.4 0.0 reduce-scatter.2.cloned.1.call-update
  49.5 0.0 copy-done.7
  49.5 0.0 copy-done.8
  49.5 0.1 select_reduce_fusion.1
  49.6 0.0 copy-done.2
  49.6 0.0 copy-start.5
  49.6 0.0 copy-start.3
  49.6 0.1 fusion.1
  49.7 0.2 copy.30
  50.0 0.2 copy-done.4
  50.1 0.2 dynamic-slice_reduce_fusion
  50.3 0.0 copy-done
  50.3 0.6 dynamic_slice.9
  50.9 0.6 iota_compare_fusion.6
  51.6 0.2 convert_reduce_fusion.1
  51.8 0.3 convolution_convert_fusion
  52.1 0.7 copy.34
  52.8 3.4 %all-to-all-start = ((bf16[4,1,128,256]{3,2,1,0:T(8,128)(2,1)}), bf16[4,1,128,256]{3,2,1,0:T(8,128)(2,1)S(1)}, u32[]{:S(2)}, u32[]{:S(2)}) async-start(bf16[4,1,128,256]{3,2,1,0:T(8,128)(2,1)} %bitcast.26), calls=%async_computation.1 | async-start | bytes 524288 | tf_op jit(solution)/shard_map/all_to_all | solution.py:74
  56.2 0.1 copy.27
  56.3 0.6 gather_fusion.2
  57.0 0.6 gather_fusion.1
  57.6 0.1 compare_and_fusion
  57.6 0.2 convert_reduce_fusion
  57.9 0.0 copy-done.5
  57.9 0.1 select_reduce_fusion
  58.0 31.2 %psum.15 = f32[256]{0:T(256)S(1)} all-reduce(f32[256]{0:T(256)S(1)} %select_reduce_fusion), channel_id=1, replica_groups=mesh['groups'=2,'rows'=4,'cols'=2,'sub'=2] {'rows','cols','sub'}, use_global_device_ids=true, to_apply=%region_3.4 | all-reduce | flops 256 | bytes 2048 | tf_op jit(solution)/shard_map/psum | solution.py:49
  89.2 0.0 copy-done.3
  89.2 0.1 copy.25
  89.3 0.1 add_select_fusion.2
  89.4 0.2 fusion.4
  89.5 0.0 all-to-all-done
  89.6 0.2 copy.32
  89.8 0.3 convolution_convert_fusion.1
  90.1 0.7 reshape.328
  90.8 0.0 reduce-scatter.2.cloned.1.call-done
  90.8 1.1 %multiply_reduce_fusion = (f32[256]{0:T(256)S(1)}, bf16[256,256]{0,1:T(8,128)(2,1)S(1)}) fusion(f32[256]{0:T(256)S(1)} %sqrt.3, f32[256,256]{0,1:T(8,128)} %reduce-scatter.2.cloned.1.call-done, bf16[256,256]{0,1:T(8,128)(2,1)S(1)} %copy.25), kind=kLoop, calls=%fused_computation.11 | loop fusion | flops 392960 | bytes 526336 | tf_op jit(solution)/shard_map/reduce_sum | solution.py:112
  91.9 0.8 copy.29
  92.6 0.6 sub.35
  (11 shorter events, 0.1 us)
Async XLA Ops:
  7.2 83.6 %reduce-scatter.2.cloned.1.call-start = ((), (), s32[]{:S(2)}) async-start(), calls=%async_computation.2 | async-start | bytes 1310720 | tf_op jit(solution)/shard_map/reduce_scatter | solution.py:101
  7.2 1.7 %copy-start.6 = (s32[256]{0:T(256)S(1)}, s32[256]{0:T(256)}, u32[]{:S(2)}) copy-start(s32[256]{0:T(256)} %param.11) | copy-start | bytes 3076
  10.2 37.6 %copy-start.1 = (bf16[768,1024]{1,0:T(8,128)(2,1)S(1)}, bf16[768,1024]{1,0:T(8,128)(2,1)}, u32[]{:S(2)}) copy-start(bf16[768,1024]{1,0:T(8,128)(2,1)} %param.9) | copy-start | bytes 4718596
  47.8 1.6 %copy-start.7 = (s32[4,128]{1,0:T(4,128)S(1)}, s32[4,128]{1,0:T(4,128)}, u32[]{:S(2)}) copy-start(s32[4,128]{1,0:T(4,128)} %param.14) | copy-start | bytes 6148
  47.8 1.6 %copy-start.8 = (f32[4]{0:T(128)S(1)}, f32[4]{0:T(128)}, u32[]{:S(2)}) copy-start(f32[4]{0:T(128)} %param.17) | copy-start | bytes 52
  47.9 1.7 %copy-start.2 = (bf16[4,128,256]{2,1,0:T(8,128)(2,1)S(1)}, bf16[4,128,256]{2,1,0:T(8,128)(2,1)}, u32[]{:S(2)}) copy-start(bf16[4,128,256]{2,1,0:T(8,128)(2,1)} %param.13) | copy-start | bytes 786436
  49.4 0.7 copy-start.4
  49.4 0.9 copy-start
  49.6 8.3 %copy-start.5 = (f32[256]{0:T(256)S(1)}, f32[256]{0:T(256)}, u32[]{:S(2)}) copy-start(f32[256]{0:T(256)} %param.12) | copy-start | bytes 3076
  49.6 39.6 %copy-start.3 = (bf16[256,256]{1,0:T(8,128)(2,1)S(1)}, bf16[256,256]{1,0:T(8,128)(2,1)}, u32[]{:S(2)}) copy-start(bf16[256,256]{1,0:T(8,128)(2,1)} %param.10) | copy-start | bytes 393220
  52.8 36.7 %all-to-all-start = ((bf16[4,1,128,256]{3,2,1,0:T(8,128)(2,1)}), bf16[4,1,128,256]{3,2,1,0:T(8,128)(2,1)S(1)}, u32[]{:S(2)}, u32[]{:S(2)}) async-start(bf16[4,1,128,256]{3,2,1,0:T(8,128)(2,1)} %bitcast.26), calls=%async_computation.1 | async-start | bytes 524288 | tf_op jit(solution)/shard_map/all_to_all | solution.py:74
Sparse Core Ops, SparseCore 0:
  49.6 24.2 reduce-scatter.1
where the time goes:
time: 100 us
  blocking collectives  68.6 us (69%)
  between operations  14.3 us (14%)
  local copies, waits for them, and re-layouts  7.74 us (8%)
  other arithmetic  3.79 us (4%)
  starting transfers between devices  3.44 us (3%)
  matrix products  2.14 us (2%)
    psum x1, blocking collectives, body(): pivot_rows = lax.psum(picked, 'rows').astype(jnp.bfloat16)  37.4 us
    psum x1, blocking collectives, body(): pivot_diag = lax.psum(diag_terms, ('rows', 'cols', 'sub'))  31.2 us
    unnamed x25, local copies, waits for them, and re-layouts  4.02 us
    all_to_all x1, starting transfers between devices, body(): lax.all_to_all(outgoing, 'rows', split_axis=0, concat_axis=0, tiled=True)  3.4 us
  transfers between devices with their start and end apart: 2, of which 0 were waited for; matrix products, arithmetic and copies ran while one was open for 6% of the time, Pallas kernels for 0%

commit v1 on v0

--- a/solution.py
+++ b/solution.py
@@ -46,7 +46,7 @@
     local_pivots = pivots - device_index * rows_here
     matches = jnp.arange(rows_here, dtype=jnp.int32)[:, None] == local_pivots[None, :]
     diag_terms = jnp.sum(jnp.where(matches, diagonal[:, None], jnp.float32(0.0)), axis=0)
-    pivot_diag = lax.psum(diag_terms, ("rows", "cols", "sub"))
+    pivot_diag = jnp.sum(lax.all_gather(diag_terms, ("rows", "cols", "sub")), axis=0)
     band_pivots = pivots - band_index * band_rows
     inside = (band_pivots >= 0) & (band_pivots < band_rows)
     clamped = jnp.clip(band_pivots, 0, band_rows - 1)

time: 100 us -> 91.1 us (0.911)
  blocking collectives: 68.6 us -> 59.3 us
    psum x1 -> x0, blocking collectives: 31.2 us -> none  [body(): pivot_diag = lax.psum(diag_terms, ('rows', 'cols', 'sub'))]
    all_gather x0 -> x1, blocking collectives: none -> 21.8 us  [body(): lax.all_gather(diag_terms, ('rows', 'cols', 'sub'))]
  transfers between devices with their start and end apart: 2 -> 2, of which waited for: 0 -> 0; matrix products, arithmetic and copies ran while one was open for 6% -> 7% of each run, Pallas kernels for 0% -> 0%
where the time goes in v1:
time: 91.1 us; the launch traced here: 90.7 us
  blocking collectives  59.3 us (65%)
  between operations  14.3 us (16%)
  local copies, waits for them, and re-layouts  7.74 us (8%)
  other arithmetic  3.83 us (4%)
  starting transfers between devices  3.44 us (4%)
  matrix products  2.14 us (2%)
    psum x1, blocking collectives, body(): pivot_rows = lax.psum(picked, 'rows').astype(jnp.bfloat16)  37.4 us
    all_gather x1, blocking collectives, body(): lax.all_gather(diag_terms, ('rows', 'cols', 'sub'))  21.8 us
    unnamed x25, local copies, waits for them, and re-layouts  4.02 us
    all_to_all x1, starting transfers between devices, body(): lax.all_to_all(outgoing, 'rows', split_axis=0, concat_axis=0, tiled=True)  3.4 us
  transfers between devices with their start and end apart: 2, of which 0 were waited for; matrix products, arithmetic and copies ran while one was open for 7% of the time, Pallas kernels for 0%

profile of v1, /device:TPU:0, one launch (start us, length us, event | category | flops | bytes accessed | tf_op | source)
XLA Modules:
  0.0 90.7 jit_solution(16961252042723225403)
XLA Ops:
  7.2 0.0 reduce-scatter.2.cloned.1.call-start
  7.2 0.0 copy-start.6
  7.2 1.7 %copy.26 = bf16[768,1024]{0,1:T(8,128)(2,1)S(1)} copy(bf16[768,1024]{1,0:T(8,128)(2,1)} %param.9) | data formatting | bytes 3145728 | tf_op args[0]
  9.0 0.0 copy-done.6
  9.0 1.2 %gather_fusion = bf16[256,768]{1,0:T(8,128)(2,1)S(1)} fusion(bf16[768,1024]{0,1:T(8,128)(2,1)S(1)} %copy.26, s32[1024]{0:T(1024)S(1)} %pad_clamp_fusion.1), kind=kCustom, calls=%fused_computation | custom fusion | bytes 787456 | tf_op jit(solution)/shard_map/jit(_take)/gather | solution.py:53
  10.2 0.0 copy-start.1
  10.2 0.2 select_bitcast_fusion
  10.4 37.4 %all-reduce.1 = bf16[768,256]{0,1:T(8,128)(2,1)S(1)} all-reduce(f32[768,256]{0,1:T(8,128)S(1)} %select_bitcast_fusion), channel_id=1, replica_groups=mesh['groups'=2,'rows'=4,'cols'=2,'sub'=2] {'rows'}, use_global_device_ids=true, to_apply=%region_0.1 | all-reduce | flops 196608 | bytes 1179648 | tf_op jit(solution)/shard_map/psum | solution.py:55
  47.8 0.0 copy-done.1
  47.8 0.0 copy-start.7
  47.8 0.0 copy-start.8
  47.9 0.0 copy-start.2
  47.9 1.6 %convolution_bitcast_fusion = f32[1024,256]{0,1:T(8,128)} fusion(bf16[768,1024]{1,0:T(8,128)(2,1)S(1)} %copy-done.1, bf16[768,256]{0,1:T(8,128)(2,1)S(1)} %all-reduce.1), kind=kOutput, calls=%fused_computation.5 | convolution fusion | flops 402653184 | bytes 3014656 | tf_op jit(solution)/shard_map/dot_general | solution.py:102
  49.4 0.0 copy-start.4
  49.4 0.0 copy-start
  49.4 0.0 reduce-scatter.2.cloned.1.call-update
  49.5 0.0 copy-done.7
  49.5 0.0 copy-done.8
  49.5 0.1 select_reduce_fusion.1
  49.6 0.0 copy-done.2
  49.6 0.0 copy-start.5
  49.6 0.0 copy-start.3
  49.6 0.1 fusion.1
  49.7 0.2 copy.30
  50.0 0.2 copy-done.4
  50.1 0.2 dynamic-slice_reduce_fusion
  50.3 0.0 copy-done
  50.3 0.6 dynamic_slice.9
  50.9 0.6 iota_compare_fusion.6
  51.6 0.2 convert_reduce_fusion.1
  51.8 0.3 convolution_convert_fusion
  52.1 0.7 copy.34
  52.8 3.4 %all-to-all-start = ((bf16[4,1,128,256]{3,2,1,0:T(8,128)(2,1)}), bf16[4,1,128,256]{3,2,1,0:T(8,128)(2,1)S(1)}, u32[]{:S(2)}, u32[]{:S(2)}) async-start(bf16[4,1,128,256]{3,2,1,0:T(8,128)(2,1)} %bitcast.27), calls=%async_computation.1 | async-start | bytes 524288 | tf_op jit(solution)/shard_map/all_to_all | solution.py:74
  56.2 0.1 copy.27
  56.3 0.6 gather_fusion.2
  57.0 0.6 gather_fusion.1
  57.6 0.1 compare_and_fusion
  57.6 0.2 convert_reduce_fusion
  57.9 0.0 copy-done.5
  57.9 0.1 select_reduce_fusion
  58.0 21.8 %all-gather.1 = f32[16,1,256]{2,1,0:T(1,128)S(1)} all-gather(f32[1,1,256]{2,1,0:T(1,128)S(1)} %bitcast.32), channel_id=2, replica_groups=mesh['groups'=2,'rows'=4,'cols'=2,'sub'=2] {'rows','cols','sub'}, dimensions={0}, use_global_device_ids=true | all-gather | bytes 17408 | tf_op jit(solution)/shard_map/all_gather | solution.py:49
  79.9 0.0 copy-done.3
  79.9 0.1 copy.25
  80.0 0.1 add_select_fusion.2
  80.1 0.2 fusion.4
  80.2 0.0 all-to-all-done
  80.2 0.2 copy.32
  80.5 0.3 convolution_convert_fusion.1
  80.7 0.7 reshape.330
  81.5 0.0 reduce-scatter.2.cloned.1.call-done
  81.5 1.1 %multiply_reduce_fusion = (f32[256]{0:T(256)S(1)}, bf16[256,256]{0,1:T(8,128)(2,1)S(1)}) fusion(f32[256]{0:T(256)S(1)} %sqrt.7, f32[256,256]{0,1:T(8,128)} %reduce-scatter.2.cloned.1.call-done, bf16[256,256]{0,1:T(8,128)(2,1)S(1)} %copy.25), kind=kLoop, calls=%fused_computation.11 | loop fusion | flops 392960 | bytes 526336 | tf_op jit(solution)/shard_map/reduce_sum | solution.py:112
  82.6 0.8 copy.29
  83.3 0.6 sub.35
  (12 shorter events, 0.1 us)
Async XLA Ops:
  7.2 74.3 %reduce-scatter.2.cloned.1.call-start = ((), (), s32[]{:S(2)}) async-start(), calls=%async_computation.2 | async-start | bytes 1310720 | tf_op jit(solution)/shard_map/reduce_scatter | solution.py:101
  7.2 1.7 %copy-start.6 = (s32[256]{0:T(256)S(1)}, s32[256]{0:T(256)}, u32[]{:S(2)}) copy-start(s32[256]{0:T(256)} %param.11) | copy-start | bytes 3076
  10.2 37.6 %copy-start.1 = (bf16[768,1024]{1,0:T(8,128)(2,1)S(1)}, bf16[768,1024]{1,0:T(8,128)(2,1)}, u32[]{:S(2)}) copy-start(bf16[768,1024]{1,0:T(8,128)(2,1)} %param.9) | copy-start | bytes 4718596
  47.8 1.6 %copy-start.7 = (s32[4,128]{1,0:T(4,128)S(1)}, s32[4,128]{1,0:T(4,128)}, u32[]{:S(2)}) copy-start(s32[4,128]{1,0:T(4,128)} %param.14) | copy-start | bytes 6148
  47.8 1.6 %copy-start.8 = (f32[4]{0:T(128)S(1)}, f32[4]{0:T(128)}, u32[]{:S(2)}) copy-start(f32[4]{0:T(128)} %param.17) | copy-start | bytes 52
  47.9 1.7 %copy-start.2 = (bf16[4,128,256]{2,1,0:T(8,128)(2,1)S(1)}, bf16[4,128,256]{2,1,0:T(8,128)(2,1)}, u32[]{:S(2)}) copy-start(bf16[4,128,256]{2,1,0:T(8,128)(2,1)} %param.13) | copy-start | bytes 786436
  49.4 0.7 copy-start.4
  49.4 0.9 copy-start
  49.6 8.3 %copy-start.5 = (f32[256]{0:T(256)S(1)}, f32[256]{0:T(256)}, u32[]{:S(2)}) copy-start(f32[256]{0:T(256)} %param.12) | copy-start | bytes 3076
  49.6 30.3 %copy-start.3 = (bf16[256,256]{1,0:T(8,128)(2,1)S(1)}, bf16[256,256]{1,0:T(8,128)(2,1)}, u32[]{:S(2)}) copy-start(bf16[256,256]{1,0:T(8,128)(2,1)} %param.10) | copy-start | bytes 393220
  52.8 27.4 %all-to-all-start = ((bf16[4,1,128,256]{3,2,1,0:T(8,128)(2,1)}), bf16[4,1,128,256]{3,2,1,0:T(8,128)(2,1)S(1)}, u32[]{:S(2)}, u32[]{:S(2)}) async-start(bf16[4,1,128,256]{3,2,1,0:T(8,128)(2,1)} %bitcast.27), calls=%async_computation.1 | async-start | bytes 524288 | tf_op jit(solution)/shard_map/all_to_all | solution.py:74
Sparse Core Ops, SparseCore 0:
  49.6 24.1 reduce-scatter.1
